TPU v7x, 32 devices: a whole 2x2x4 slice. The times are simulated.
32 devices in a mesh: node: 8 (over z, y), local: 4 (over x, core).
Axes of the slice: x: 2, y: 2, z: 4, core: 2. Of those that a mesh axis runs over, the one named last changes fastest.
Arguments:
- tokens: bfloat16 [4096, 7168], P(('node', 'local')), may hold values from -6 to 6
- w_gate: bfloat16 [8, 7168, 1024], P('node', None, 'local'), may hold values from -0.0625 to 0.0625
- w_up: bfloat16 [8, 7168, 1024], P('node', None, 'local'), may hold values from -0.0625 to 0.0625
- w_down: bfloat16 [8, 1024, 7168], P('node', 'local'), may hold values from -0.1875 to 0.1875
- chosen: int32 [8, 48], replicated, may hold values from 0 to 4095, as said below
- counts: int32 [8], replicated, may hold values from 3 to 48, as said below
- gates: float32 [8, 48], replicated, may hold values from 0.2 to 1
Outputs:
- mixed: bfloat16 [4096, 7168], P(('node', 'local'))
Inputs may be any that keep to these rules, and one draw needn't show every extreme that they name: `chosen`: each expert's list holds distinct tokens; in each list at most 3 entries lie in one device's block of 128 consecutive tokens, and for every expert some block holds exactly 3 live entries. `counts`: some expert has exactly 48 live entries.
All inputs are finite; a program needn't handle non-finite values.
Results may differ from a plain program's by a relative error of at most 0.014.
Values may be sent and summed in bfloat16 or wider, within the bound.
A program may use at most 128 MiB of HBM per device.

v0:
```python
import jax
import jax.numpy as jnp
from jax import lax
from jax.sharding import PartitionSpec as P

SLOT = 3


def shards(tokens, w_gate, w_up, w_down, chosen, counts, gates):
    tok_dev = tokens.shape[0]
    width = tokens.shape[1]
    n_node = lax.axis_size("node")
    n_local = lax.axis_size("local")
    devices = n_node * n_local
    cap = chosen.shape[1]
    experts = chosen.shape[0]
    myself = lax.axis_index("node") * n_local + lax.axis_index("local")
    live = jnp.arange(cap, dtype=jnp.int32)[None, :] < counts[:, None]
    owner = chosen // tok_dev
    mine = live & (owner == myself)
    rank = jnp.cumsum(mine.astype(jnp.int32), axis=1) - 1
    select = (
        mine[:, :, None] & (rank[:, :, None] == jnp.arange(SLOT, dtype=jnp.int32)[None, None, :])
    ).astype(jnp.int32)
    position = chosen - owner * tok_dev
    token_slot = jnp.sum(select * position[:, :, None], axis=1)
    present = jnp.sum(select, axis=1)
    outgoing = tokens[token_slot.reshape(-1)].reshape(experts, SLOT, width)
    outgoing = outgoing * present[:, :, None].astype(jnp.bfloat16)
    expert = lax.axis_index("node")
    picked = lax.dynamic_index_in_dim(chosen, expert, 0, keepdims=False)
    count = lax.dynamic_index_in_dim(counts, expert, 0, keepdims=False)
    weight = lax.dynamic_index_in_dim(gates, expert, 0, keepdims=False)
    valid = jnp.arange(cap, dtype=jnp.int32) < count
    holder = picked // tok_dev
    member = (
        (holder[:, None] == jnp.arange(devices, dtype=jnp.int32)[None, :]) & valid[:, None]
    ).astype(jnp.int32)
    order_in = jnp.sum(member * jnp.cumsum(member, axis=0), axis=1) - 1
    column = holder * SLOT + order_in
    table = jnp.sum(
        jnp.where(
            valid[:, None]
            & (column[:, None] == jnp.arange(devices * SLOT, dtype=jnp.int32)[None, :]),
            weight[:, None],
            jnp.float32(0.0),
        ),
        axis=0,
    )
    table = table.reshape(n_node, n_local, SLOT).transpose(1, 0, 2)
    gate_mat = w_gate[0]
    up_mat = w_up[0]
    down_mat = w_down[0]
    ff_dev = gate_mat.shape[1]
    arrived = lax.all_to_all(outgoing, "node", split_axis=0, concat_axis=0, tiled=True)
    piece = lax.all_gather(arrived[None], "local", axis=0, tiled=True)
    flat = piece.reshape(-1, width)
    gate_val = jnp.dot(flat, gate_mat, preferred_element_type=jnp.float32)
    up_val = jnp.dot(flat, up_mat, preferred_element_type=jnp.float32)
    hidden = (jax.nn.silu(gate_val) * up_val).astype(jnp.bfloat16)
    down_hidden = hidden.reshape(piece.shape[0], n_node, SLOT, ff_dev)
    count_rows = down_hidden.shape[0]
    down_val = jnp.dot(
        down_hidden.reshape(-1, ff_dev), down_mat, preferred_element_type=jnp.float32
    )
    down_val = down_val.reshape(count_rows, n_node, SLOT, width)
    partial_value = (down_val * table[:, :, :, None]).astype(jnp.bfloat16)
    summed = lax.psum_scatter(
        partial_value.astype(jnp.float32).astype(jnp.bfloat16),
        "local",
        scatter_dimension=0,
        tiled=True,
    )
    returned = lax.all_to_all(summed, "node", split_axis=1, concat_axis=1, tiled=True)
    answers = returned[0].reshape(experts * SLOT, width)
    placing = (jnp.arange(tok_dev, dtype=jnp.int32)[:, None] == token_slot.reshape(-1)[None, :]) & (
        present.reshape(-1)[None, :] > 0
    )
    mixed = jnp.dot(placing.astype(jnp.bfloat16), answers, preferred_element_type=jnp.float32)
    return mixed.astype(jnp.bfloat16)


def solution(mesh):
    in_specs = (
        P(("node", "local"), None),
        P("node", None, "local"),
        P("node", None, "local"),
        P("node", "local", None),
        P(),
        P(),
        P(),
    )
    out_specs = P(("node", "local"), None)
    return jax.shard_map(shards, mesh=mesh, in_specs=in_specs, out_specs=out_specs, check_vma=False)
```

profile of v0, /device:TPU:0, one launch (start us, length us, event | category | flops | bytes accessed | tf_op | source)
XLA Modules:
  0.0 119.9 jit_solution(16415027315541604071)
XLA Ops:
  6.5 0.9 fusion.25
  7.6 0.7 multiply_subtract_fusion
  8.7 0.8 gather_fusion
  9.8 0.3 broadcast_multiply_fusion
  10.1 20.3 %all_to_all.10 = bf16[8,3,7168]{2,1,0:T(4,128)(2,1)S(1)} all-to-all(bf16[8,3,7168]{2,1,0:T(4,128)(2,1)S(1)} %broadcast_multiply_fusion), channel_id=1, replica_groups=mesh['node'=8,'local'=4] {'node'}, dimensions={0} | all-to-all | bytes 688128 | tf_op jit(solution)/shard_map/all_to_all | solution.py:55
  30.4 0.9 copy.22
  31.3 0.6 dynamic_slice.12
  32.0 0.7 and_select_fusion
  32.6 0.6 iota_compare_fusion.5
  33.5 0.7 dynamic-slice_bitcast_fusion
  34.3 0.7 add_add_fusion
  35.4 13.7 %all-gather.3.cloned.1.call-done = bf16[32,3,7168]{2,0,1:T(8,128)(2,1)} async-done(((bf16[8,3,7168]{2,0,1:T(8,128)(2,1)}), bf16[32,3,7168]{2,0,1:T(8,128)(2,1)}) %all-gather.3.cloned.1.call-update) | async-done | bytes 1376272 | tf_op jit(solution)/shard_map/all_gather | solution.py:56
  49.0 3.7 %copy.23 = bf16[32,3,7168]{2,1,0:T(4,128)(2,1)} copy(bf16[32,3,7168]{2,0,1:T(8,128)(2,1)} %all-gather.3.cloned.1.call-done) | data formatting | bytes 2752512 | tf_op jit(solution)/shard_map/all_gather | solution.py:56
  52.8 3.0 %reshape.117 = bf16[96,7168]{1,0:T(8,128)(2,1)S(1)} reshape(bf16[32,3,7168]{2,1,0:T(4,128)(2,1)} %copy.23) | data formatting | bytes 2752512 | tf_op jit(solution)/shard_map/reshape | solution.py:57
  55.8 2.9 %fusion.4 = f32[96,256]{1,0:T(8,128)S(1)} fusion(bf16[96,7168]{1,0:T(8,128)(2,1)S(1)} %reshape.117, bf16[1,7168,256]{2,1,0:T(8,128)(2,1)} %param.8), kind=kOutput, calls=%fused_computation.7 | convolution fusion | flops 352321536 | bytes 5144576 | tf_op jit(solution)/shard_map/dot_general | solution.py:58
  58.7 0.2 copy-done.1
  58.9 0.7 fusion.9
  59.7 3.8 %fusion = bf16[4,8,3,7168]{3,1,2,0:T(8,128)(2,1)} fusion(bf16[1,256,7168]{2,1,0:T(8,128)(2,1)} %param.10, f32[4,8,3]{1,2,0:T(4,128)S(1)} %copy.25, bf16[4,8,3,256]{3,2,1,0:T(4,128)(2,1)S(1)} %dot_general.16), kind=kOutput, calls=%fused_computation.3 | convolution fusion | flops 353697792 | bytes 5095808 | tf_op jit(solution)/shard_map/dot_general | solution.py:63
  63.6 26.9 %reduce-scatter.2.cloned.1.call-done = bf16[1,8,3,7168]{3,1,2,0:T(8,128)(2,1)} async-done(((bf16[4,8,3,7168]{3,1,2,0:T(8,128)(2,1)}), bf16[1,8,3,7168]{3,1,2,0:T(8,128)(2,1)}) %reduce-scatter.2.cloned.1.call-update) | async-done | bytes 344080 | tf_op jit(solution)/shard_map/reduce_scatter | solution.py:68
  90.4 2.0 %copy.26 = bf16[1,8,3,7168]{3,2,0,1:T(4,128)(2,1)} copy(bf16[1,8,3,7168]{3,1,2,0:T(8,128)(2,1)} %reduce-scatter.2.cloned.1.call-done) | data formatting | bytes 688128 | tf_op jit(solution)/shard_map/reduce_scatter | solution.py:68
  92.5 5.5 %all-to-all-start.1 = ((bf16[1,8,3,7168]{3,2,0,1:T(4,128)(2,1)}), bf16[1,8,3,7168]{3,2,0,1:T(4,128)(2,1)S(1)}, u32[]{:S(2)}, u32[]{:S(2)}) async-start(bf16[1,8,3,7168]{3,2,0,1:T(4,128)(2,1)} %copy.26), calls=%async_computation.2 | async-start | bytes 917504 | tf_op jit(solution)/shard_map/all_to_all | solution.py:74
  98.3 12.7 %all-to-all-done.1 = bf16[1,8,3,7168]{3,2,0,1:T(4,128)(2,1)S(1)} async-done(((bf16[1,8,3,7168]{3,2,0,1:T(4,128)(2,1)}), bf16[1,8,3,7168]{3,2,0,1:T(4,128)(2,1)S(1)}, u32[]{:S(2)}, u32[]{:S(2)}) %all-to-all-start.1) | async-done | bytes 344096 | tf_op jit(solution)/shard_map/all_to_all | solution.py:74
  110.9 0.3 reshape_squeeze.3
  111.2 1.9 %convolution_convert_fusion = bf16[128,7168]{1,0:T(8,128)(2,1)} fusion(bf16[24,7168]{1,0:T(8,128)(2,1)S(1)} %reshape_squeeze.3, s32[24]{0:T(128)S(1)} %eq.66, pred[24]{0:T(512)(128)(4,1)S(1)} %gt.12), kind=kOutput, calls=%fused_computation.1 | convolution fusion | flops 44963840 | bytes 2179192 | tf_op jit(solution)/shard_map/dot_general | solution.py:79
  (29 shorter events, 1.9 us)
Async XLA Ops:
  6.5 2.2 %copy-start = (bf16[128,7168]{1,0:T(8,128)(2,1)S(1)}, bf16[128,7168]{1,0:T(8,128)(2,1)}, u32[]{:S(2)}) copy-start(bf16[128,7168]{1,0:T(8,128)(2,1)} %param.7) | copy-start | bytes 5505028
  6.5 42.5 %all-gather.3.cloned.1.call-start = ((), (), s32[]{:S(2)}) async-start(), calls=%async_computation.4 | async-start | bytes 1720320 | tf_op jit(solution)/shard_map/all_gather | solution.py:56
  8.7 22.6 %copy-start.2 = (s32[8]{0:T(128)S(1)}, s32[8]{0:T(128)}, u32[]{:S(2)}) copy-start(s32[8]{0:T(128)} %param.12) | copy-start | bytes 100
  31.3 59.2 %reduce-scatter.2.cloned.1.call-start = ((), (), s32[]{:S(2)}) async-start(), calls=%async_computation.3 | async-start | bytes 1720320 | tf_op jit(solution)/shard_map/reduce_scatter | solution.py:68
  55.8 3.1 %copy-start.1 = (bf16[1,7168,256]{2,1,0:T(8,128)(2,1)S(1)}, bf16[1,7168,256]{2,1,0:T(8,128)(2,1)}, u32[]{:S(2)}) copy-start(bf16[1,7168,256]{2,1,0:T(8,128)(2,1)} %param.9) | copy-start | bytes 11010052
  92.5 18.4 %all-to-all-start.1 = ((bf16[1,8,3,7168]{3,2,0,1:T(4,128)(2,1)}), bf16[1,8,3,7168]{3,2,0,1:T(4,128)(2,1)S(1)}, u32[]{:S(2)}, u32[]{:S(2)}) async-start(bf16[1,8,3,7168]{3,2,0,1:T(4,128)(2,1)} %copy.26), calls=%async_computation.2 | async-start | bytes 917504 | tf_op jit(solution)/shard_map/all_to_all | solution.py:74
Sparse Core Ops, SparseCore 0:
  31.4 17.5 all-gather.2
  63.7 26.7 reduce-scatter.1
where the time goes:
time: 120 us
  waiting for transfers between devices  53.3 us (44%)
  blocking collectives  20.3 us (17%)
  between operations  13.5 us (11%)
  local copies, waits for them, and re-layouts  13.2 us (11%)
  matrix products  9.34 us (8%)
  starting transfers between devices  5.55 us (5%)
  other arithmetic  4.75 us (4%)
    reduce_scatter x1, waiting for transfers between devices, shards(): lax.psum_scatter(partial_value.astype(jnp.float32).astype(jnp.bfloat16),...  26.9 us
    all_to_all x1, blocking collectives, shards(): lax.all_to_all(outgoing, 'node', split_axis=0, concat_axis=0, tiled=True)  20.3 us
    all_gather x1, waiting for transfers between devices, shards(): piece = lax.all_gather(arrived[None], 'local', axis=0, tiled=True)  13.7 us
    all_to_all x1, waiting for transfers between devices, shards(): lax.all_to_all(summed, 'node', split_axis=1, concat_axis=1, tiled=True)  12.7 us
    all_to_all x1, starting transfers between devices, shards(): lax.all_to_all(summed, 'node', split_axis=1, concat_axis=1, tiled=True)  5.51 us
    dot_general x1, matrix products, shards(): jnp.dot(down_hidden.reshape(-1, ff_dev), down_mat, preferred_element_type...  3.84 us
    all_gather x1, local copies, waits for them, and re-layouts, shards(): piece = lax.all_gather(arrived[None], 'local', axis=0, tiled=True)  3.75 us
    reshape x1, local copies, waits for them, and re-layouts, shards(): flat = piece.reshape(-1, width)  2.97 us
  transfers between devices with their start and end apart: 3, of which 3 were waited for; matrix products, arithmetic and copies ran while one was open for 4% of the time, Pallas kernels for 0%

commit v1 on v0

--- a/solution.py
+++ b/solution.py
@@ -53,7 +53,14 @@
     down_mat = w_down[0]
     ff_dev = gate_mat.shape[1]
     arrived = lax.all_to_all(outgoing, "node", split_axis=0, concat_axis=0, tiled=True)
-    piece = lax.all_gather(arrived[None], "local", axis=0, tiled=True)
+    ring = [arrived[None]]
+    for hop in range(3):
+        ring.append(lax.ppermute(ring[-1], "local", [(dev, (dev + 1) % 4) for dev in range(4)]))
+    piece = jnp.roll(
+        jnp.concatenate(ring[::-1], axis=0),
+        (lax.axis_index("local") + 1) * ring[0].shape[0],
+        axis=0,
+    )
     flat = piece.reshape(-1, width)
     gate_val = jnp.dot(flat, gate_mat, preferred_element_type=jnp.float32)
     up_val = jnp.dot(flat, up_mat, preferred_element_type=jnp.float32)

time: 120 us -> 126 us (1.050)
  waiting for transfers between devices: 53.3 us -> 58.4 us
    ppermute x0 -> x3, waiting for transfers between devices: none -> 19.8 us  [shards(): lax.ppermute(ring[-1], 'local', [(dev, (dev + 1) % 4) for dev in range(4)])]
    all_gather x1 -> x0, waiting for transfers between devices: 13.7 us -> none  [shards(): piece = lax.all_gather(arrived[None], 'local', axis=0, tiled=True)]
    all_gather x1 -> x0, local copies, waits for them, and re-layouts: 3.75 us -> none  [shards(): piece = lax.all_gather(arrived[None], 'local', axis=0, tiled=True)]
    unnamed x6 -> x13, local copies, waits for them, and re-layouts: 0.24 us -> 3.58 us
    dynamic_slice x0 -> x1, local copies, waits for them, and re-layouts: none -> 1.91 us  [shards(): jnp.roll(jnp.concatenate(ring[::-1], axis=0), (lax.axis_index('local') +...]
  transfers between devices with their start and end apart: 3 -> 5, of which waited for: 3 -> 5; matrix products, arithmetic and copies ran while one was open for 4% -> 3% of each run, Pallas kernels for 0% -> 0%
where the time goes in v1:
time: 126 us
  waiting for transfers between devices  58.4 us (46%)
  blocking collectives  20.3 us (16%)
  local copies, waits for them, and re-layouts  14 us (11%)
  between operations  13.5 us (11%)
  matrix products  9.34 us (7%)
  starting transfers between devices  5.53 us (4%)
  other arithmetic  4.75 us (4%)
    reduce_scatter x1, waiting for transfers between devices, shards(): lax.psum_scatter(partial_value.astype(jnp.float32).astype(jnp.bfloat16),...  25.9 us
    all_to_all x1, blocking collectives, shards(): lax.all_to_all(outgoing, 'node', split_axis=0, concat_axis=0, tiled=True)  20.3 us
    ppermute x3, waiting for transfers between devices, shards(): lax.ppermute(ring[-1], 'local', [(dev, (dev + 1) % 4) for dev in range(4)])  19.8 us
    all_to_all x1, waiting for transfers between devices, shards(): lax.all_to_all(summed, 'node', split_axis=1, concat_axis=1, tiled=True)  12.7 us
    all_to_all x1, starting transfers between devices, shards(): lax.all_to_all(summed, 'node', split_axis=1, concat_axis=1, tiled=True)  5.52 us
    dot_general x1, matrix products, shards(): jnp.dot(down_hidden.reshape(-1, ff_dev), down_mat, preferred_element_type...  3.84 us
    unnamed x13, local copies, waits for them, and re-layouts  3.58 us
    reshape x1, local copies, waits for them, and re-layouts, shards(): flat = piece.reshape(-1, width)  2.97 us
  transfers between devices with their start and end apart: 5, of which 5 were waited for; matrix products, arithmetic and copies ran while one was open for 3% of the time, Pallas kernels for 0%

profile of v1, /device:TPU:0, one launch (start us, length us, event | category | flops | bytes accessed | tf_op | source)
XLA Modules:
  0.0 125.8 jit_solution(15514868085279137015)
XLA Ops:
  6.5 0.9 fusion.27
  7.6 0.7 multiply_subtract_fusion
  8.7 0.8 gather_fusion
  10.1 20.3 %all_to_all.10 = bf16[8,3,7168]{2,1,0:T(4,128)(2,1)S(1)} all-to-all(bf16[8,3,7168]{2,1,0:T(4,128)(2,1)S(1)} %broadcast_multiply_fusion), channel_id=1, replica_groups=mesh['node'=8,'local'=4] {'node'}, dimensions={0} | all-to-all | bytes 688128 | tf_op jit(solution)/shard_map/all_to_all | solution.py:55
  30.4 0.6 dynamic_slice.17
  31.0 0.7 and_select_fusion
  31.7 6.6 %collective-permute-done = bf16[1,8,3,7168]{3,2,1,0:T(4,128)(2,1)S(1)} collective-permute-done((bf16[1,8,3,7168]{3,2,1,0:T(4,128)(2,1)S(1)}, bf16[1,8,3,7168]{3,2,1,0:T(4,128)(2,1)S(1)}, u32[]{:S(2)}, u32[]{:S(2)}) %collective-permute-start) | collective-permute-done | bytes 344096 | tf_op jit(solution)/shard_map/ppermute | solution.py:58
  38.3 0.7 iota_compare_fusion.5
  39.3 6.9 %collective-permute-done.1 = bf16[1,8,3,7168]{3,2,1,0:T(4,128)(2,1)S(1)} collective-permute-done((bf16[1,8,3,7168]{3,2,1,0:T(4,128)(2,1)S(1)}, bf16[1,8,3,7168]{3,2,1,0:T(4,128)(2,1)S(1)}, u32[]{:S(2)}, u32[]{:S(2)}) %collective-permute-start.1) | collective-permute-done | bytes 344096 | tf_op jit(solution)/shard_map/ppermute | solution.py:58
  46.2 0.7 fusion.25
  46.9 0.7 add_add_fusion
  47.9 6.3 %collective-permute-done.2 = bf16[1,8,3,7168]{3,2,1,0:T(4,128)(2,1)} collective-permute-done((bf16[1,8,3,7168]{3,2,1,0:T(4,128)(2,1)S(1)}, bf16[1,8,3,7168]{3,2,1,0:T(4,128)(2,1)}, u32[]{:S(2)}, u32[]{:S(2)}) %collective-permute-start.2) | collective-permute-done | bytes 344096 | tf_op jit(solution)/shard_map/ppermute | solution.py:58
  54.2 1.2 constant_dynamic-update-slice_fusion.7
  56.0 1.2 constant_dynamic-update-slice_fusion.3
  57.8 1.9 %constant_dynamic-slice_fusion.2 = bf16[4,8,3,7168]{3,2,1,0:T(4,128)(2,1)} fusion(bf16[8,8,3,7168]{3,2,1,0:T(4,128)(2,1)S(1)} %constant_dynamic-update-slice_fusion, s32[]{:T(128)S(6)} %select_n.55), kind=kLoop, calls=%fused_computation.56 | loop fusion | bytes 2752516 | tf_op jit(solution)/shard_map/jit(_roll_dynamic)/dynamic_slice | solution.py:59
  59.7 3.0 %reshape.117 = bf16[96,7168]{1,0:T(8,128)(2,1)S(1)} reshape(bf16[4,8,3,7168]{3,2,1,0:T(4,128)(2,1)} %constant_dynamic-slice_fusion.2) | data formatting | bytes 2752512 | tf_op jit(solution)/shard_map/reshape | solution.py:64
  62.7 2.9 %fusion.4 = f32[96,256]{1,0:T(8,128)S(1)} fusion(bf16[96,7168]{1,0:T(8,128)(2,1)S(1)} %reshape.117, bf16[1,7168,256]{2,1,0:T(8,128)(2,1)} %param.8), kind=kOutput, calls=%fused_computation.7 | convolution fusion | flops 352321536 | bytes 5144576 | tf_op jit(solution)/shard_map/dot_general | solution.py:65
  65.8 0.7 fusion.9
  66.6 3.8 %fusion = bf16[4,8,3,7168]{3,1,2,0:T(8,128)(2,1)} fusion(bf16[1,256,7168]{2,1,0:T(8,128)(2,1)} %param.10, f32[4,8,3]{1,2,0:T(4,128)S(1)} %copy.21, bf16[4,8,3,256]{3,2,1,0:T(4,128)(2,1)S(1)} %dot_general.16), kind=kOutput, calls=%fused_computation.3 | convolution fusion | flops 353697792 | bytes 5095808 | tf_op jit(solution)/shard_map/dot_general | solution.py:70
  70.4 25.9 %reduce-scatter.2.cloned.1.call-done = bf16[1,8,3,7168]{3,1,2,0:T(8,128)(2,1)} async-done(((bf16[4,8,3,7168]{3,1,2,0:T(8,128)(2,1)}), bf16[1,8,3,7168]{3,1,2,0:T(8,128)(2,1)}) %reduce-scatter.2.cloned.1.call-update) | async-done | bytes 344080 | tf_op jit(solution)/shard_map/reduce_scatter | solution.py:75
  96.3 2.0 %copy.22 = bf16[1,8,3,7168]{3,2,0,1:T(4,128)(2,1)} copy(bf16[1,8,3,7168]{3,1,2,0:T(8,128)(2,1)} %reduce-scatter.2.cloned.1.call-done) | data formatting | bytes 688128 | tf_op jit(solution)/shard_map/reduce_scatter | solution.py:75
  98.4 5.5 %all-to-all-start.1 = ((bf16[1,8,3,7168]{3,2,0,1:T(4,128)(2,1)}), bf16[1,8,3,7168]{3,2,0,1:T(4,128)(2,1)S(1)}, u32[]{:S(2)}, u32[]{:S(2)}) async-start(bf16[1,8,3,7168]{3,2,0,1:T(4,128)(2,1)} %copy.22), calls=%async_computation.2 | async-start | bytes 917504 | tf_op jit(solution)/shard_map/all_to_all | solution.py:81
  104.2 12.7 %all-to-all-done.1 = bf16[1,8,3,7168]{3,2,0,1:T(4,128)(2,1)S(1)} async-done(((bf16[1,8,3,7168]{3,2,0,1:T(4,128)(2,1)}), bf16[1,8,3,7168]{3,2,0,1:T(4,128)(2,1)S(1)}, u32[]{:S(2)}, u32[]{:S(2)}) %all-to-all-start.1) | async-done | bytes 344096 | tf_op jit(solution)/shard_map/all_to_all | solution.py:81
  117.1 1.9 %convolution_convert_fusion = bf16[128,7168]{1,0:T(8,128)(2,1)} fusion(bf16[24,7168]{1,0:T(8,128)(2,1)S(1)} %reshape_squeeze.3, s32[24]{0:T(128)S(1)} %eq.69, pred[24]{0:T(512)(128)(4,1)S(1)} %gt.12), kind=kOutput, calls=%fused_computation.1 | convolution fusion | flops 44963840 | bytes 2179192 | tf_op jit(solution)/shard_map/dot_general | solution.py:86
  (39 shorter events, 3.8 us)
Async XLA Ops:
  6.5 2.2 %copy-start = (bf16[128,7168]{1,0:T(8,128)(2,1)S(1)}, bf16[128,7168]{1,0:T(8,128)(2,1)}, u32[]{:S(2)}) copy-start(bf16[128,7168]{1,0:T(8,128)(2,1)} %param.7) | copy-start | bytes 5505028
  6.5 23.8 %copy-start.2 = (s32[8]{0:T(128)S(1)}, s32[8]{0:T(128)}, u32[]{:S(2)}) copy-start(s32[8]{0:T(128)} %param.12) | copy-start | bytes 100
  6.5 89.8 %reduce-scatter.2.cloned.1.call-start = ((), (), s32[]{:S(2)}) async-start(), calls=%async_computation.3 | async-start | bytes 1720320 | tf_op jit(solution)/shard_map/reduce_scatter | solution.py:75
  30.4 7.9 %collective-permute-start = (bf16[1,8,3,7168]{3,2,1,0:T(4,128)(2,1)S(1)}, bf16[1,8,3,7168]{3,2,1,0:T(4,128)(2,1)S(1)}, u32[]{:S(2)}, u32[]{:S(2)}) collective-permute-start(bf16[1,8,3,7168]{3,2,1,0:T(4,128)(2,1)S(1)} %bitcast.37), channel_id=1, source_target_pairs={{0,1},{1,2},{2,3},{3,0},{4,5},{5,6},{6,7},{7,4},{8,9},{9,10},{10,1... | collective-permute-start | bytes 1032200 | tf_op jit(solution)/shard_map/ppermute | solution.py:58
  38.3 7.9 %collective-permute-start.1 = (bf16[1,8,3,7168]{3,2,1,0:T(4,128)(2,1)S(1)}, bf16[1,8,3,7168]{3,2,1,0:T(4,128)(2,1)S(1)}, u32[]{:S(2)}, u32[]{:S(2)}) collective-permute-start(bf16[1,8,3,7168]{3,2,1,0:T(4,128)(2,1)S(1)} %collective-permute-done), channel_id=1, source_target_pairs={{0,1},{1,2},{2,3},{3,0},{4,5},{5,6},{6,7},{7,4},{8,9},{9,10},{10,1... | collective-permute-start | bytes 1032200 | tf_op jit(solution)/shard_map/ppermute | solution.py:58
  46.2 8.0 %collective-permute-start.2 = (bf16[1,8,3,7168]{3,2,1,0:T(4,128)(2,1)S(1)}, bf16[1,8,3,7168]{3,2,1,0:T(4,128)(2,1)}, u32[]{:S(2)}, u32[]{:S(2)}) collective-permute-start(bf16[1,8,3,7168]{3,2,1,0:T(4,128)(2,1)S(1)} %collective-permute-done.1), channel_id=1, source_target_pairs={{0,1},{1,2},{2,3},{3,0},{4,5},{5,6},{6,7},{7,4},{8,9},{9,10},{10,1... | collective-permute-start | bytes 1032200 | tf_op jit(solution)/shard_map/ppermute | solution.py:58
  62.6 3.1 %copy-start.1 = (bf16[1,7168,256]{2,1,0:T(8,128)(2,1)S(1)}, bf16[1,7168,256]{2,1,0:T(8,128)(2,1)}, u32[]{:S(2)}) copy-start(bf16[1,7168,256]{2,1,0:T(8,128)(2,1)} %param.9) | copy-start | bytes 11010052
  98.4 18.5 %all-to-all-start.1 = ((bf16[1,8,3,7168]{3,2,0,1:T(4,128)(2,1)}), bf16[1,8,3,7168]{3,2,0,1:T(4,128)(2,1)S(1)}, u32[]{:S(2)}, u32[]{:S(2)}) async-start(bf16[1,8,3,7168]{3,2,0,1:T(4,128)(2,1)} %copy.22), calls=%async_computation.2 | async-start | bytes 917504 | tf_op jit(solution)/shard_map/all_to_all | solution.py:81
Sparse Core Ops, SparseCore 0:
  70.5 25.7 reduce-scatter.1
